TPU v7x, 32 devices: a whole 2x2x4 slice. The times are simulated.
32 devices in a mesh: gossip: 16 (over z, y, core), mp: 2 (over x).
Axes of the slice: x: 2, y: 2, z: 4, core: 2. Of those that a mesh axis runs over, the one named last changes fastest.
Arguments:
- params: float32 [16, 1024, 4096], P('gossip', None, 'mp'), may hold values from -6 to 6
- public: float32 [16, 1024, 64], P('gossip'), may hold values from -12 to 12
- gradients: bfloat16 [2, 16, 1024, 4096], P(None, 'gossip', None, 'mp'), may hold values from -130 to 130
- projection: float32 [4096, 64], P('mp'), may hold values from -0.09375 to 0.09375
- partners: int32 [2, 16], P(None, 'gossip'), may hold values from 0 to 15, as said below
Outputs:
- params_out: float32 [16, 1024, 4096], P('gossip', None, 'mp')
- public_out: float32 [16, 1024, 64], P('gossip')
- consensus: float32 [2], replicated
- grad_norm: float32 [2], replicated
Inputs may be any that keep to these rules, and one draw needn't show every extreme that they name: Each row is a pairing of the 16 replicas: partners[r, partners[r, i]] = i and partners[r, i] != i.
All inputs are finite; a program needn't handle non-finite values.
Results may differ from a plain program's by a relative error of at most 0.008.
Values may be sent and summed in bfloat16 or wider, within the bound.
A program may use at most 64 MiB of HBM per device.

v0:
```python
import jax
import jax.numpy as jnp
from jax import lax
from jax.sharding import PartitionSpec as P

ROUNDS = 2
step_size = 1.0
clip_limit = 0.5
mixing = 0.4
epsilon = 1e-06


def partner_rows(outgoing, table_row):
    initial = outgoing.shape
    entries = outgoing.size
    replicas = lax.axis_size("gossip")
    pieces = outgoing.reshape(replicas, entries // replicas)
    spread = lax.all_to_all(pieces, "gossip", split_axis=0, concat_axis=0, tiled=True)
    reordered = jnp.take(spread, table_row, axis=0)
    back = lax.all_to_all(reordered, "gossip", split_axis=0, concat_axis=0, tiled=True)
    return back.reshape(initial)


def body(params, public, gradients, projection, partners):
    highest = lax.Precision.HIGHEST
    mp_count = lax.axis_size("mp")
    row_count = params.shape[1]
    total = lax.axis_size("gossip") * row_count * projection.shape[0] * mp_count
    weights = params[0]
    public_state = public[0]
    drift_list = []
    norm_list = []
    whole_table = lax.all_gather(partners, "gossip", axis=1, tiled=True)
    for round_index in range(ROUNDS):
        grad_local = gradients[round_index, 0].astype(jnp.float32)
        local_squares = jnp.sum(grad_local * grad_local)
        squares = lax.psum(local_squares, ("gossip", "mp"))
        norm_value = jnp.sqrt(squares / total + epsilon)
        norm_list.append(norm_value)
        scale = jnp.minimum(1.0, clip_limit / norm_value)
        half = weights - step_size * scale * grad_local
        table_row = whole_table[round_index]
        coef_rows = public_state
        rebuilt = jnp.dot(coef_rows, projection.T, precision=highest)
        summed = lax.psum(jnp.dot(half - rebuilt, projection, precision=highest), "mp")
        sent = (public_state + summed).astype(jnp.bfloat16)
        mate = partner_rows(sent, table_row)
        public_state = sent.astype(jnp.float32)
        drift = jnp.dot(mate.astype(jnp.float32) - public_state, projection.T, precision=highest)
        weights = half + mixing * drift
        local_drift = jnp.sum(drift * drift)
        drift_list.append(lax.psum(local_drift, ("gossip", "mp")) / total)
    return (weights[None], public_state[None], jnp.stack(drift_list), jnp.stack(norm_list))


def solution(mesh):
    return jax.shard_map(
        body,
        mesh=mesh,
        in_specs=(
            P("gossip", None, "mp"),
            P("gossip", None, None),
            P(None, "gossip", None, "mp"),
            P("mp", None),
            P(None, "gossip"),
        ),
        out_specs=(P("gossip", None, "mp"), P("gossip", None, None), P(), P()),
        check_vma=False,
    )
```

profile of v0, /device:TPU:12, one launch (start us, length us, event | category | flops | bytes accessed | tf_op | source)
XLA Modules:
  0.0 274.4 jit_solution(1007616994653139488)
XLA Ops:
  7.2 5.2 %fusion.3 = (f32[]{:T(128)}, f32[]{:T(128)}) fusion(bf16[2,1,1024,2048]{3,2,1,0:T(8,128)(2,1)} %param.9), kind=kLoop, calls=%fused_computation.9 | loop fusion | flops 12582910 | bytes 8388616 | tf_op jit(solution)/shard_map/reduce_sum | solution.py:36
  12.4 41.6 %all-reduce.1 = (f32[]{:T(128)}, f32[]{:T(128)}) all-reduce(f32[]{:T(128)} %get-tuple-element.6, f32[]{:T(128)} %get-tuple-element.5), channel_id=1, replica_groups=mesh['gossip'=16,'mp'=2] {'gossip','mp'}, use_global_device_ids=true, to_apply=%region_1.0 | all-reduce | flops 2 | bytes 16 | tf_op jit(solution)/shard_map/psum | solution.py:37
  54.8 6.7 %fusion.16 = f32[1024,2048]{1,0:T(8,128)S(1)} fusion(f32[2048,64]{0,1:T(8,128)S(1)} %copy-done, f32[1,1024,64]{1,2,0:T(8,128)S(1)} %copy-done.2), kind=kOutput, calls=%fused_computation.29 | convolution fusion | flops 1610612736 | bytes 9175040 | tf_op jit(solution)/shard_map/dot_general | solution.py:44
  61.6 12.9 %fusion.8 = f32[1024,64]{0,1:T(8,128)} fusion(f32[2048,64]{0,1:T(8,128)S(1)} %copy-done, f32[1024,2048]{1,0:T(8,128)S(1)} %fusion.16, f32[1,1024,2048]{2,1,0:T(8,128)} %param.7, f32[]{:T(128)S(6)} %min.6, bf16[2,1,1024,2048]{3,2,1,0:T(8,128)(2,1)} %param.9), kind=kOutput, calls=%fused_computation.17 | convolution fusion | flops 1619001344 | bytes 21757956 | tf_op jit(solution)/shard_map/dot_general | solution.py:45
  75.2 14.1 %all-gather = s32[16,1,2]{2,1,0:T(1,128)S(1)} all-gather(s32[1,1,2]{2,1,0:T(1,128)S(1)} %bitcast.64), channel_id=1, replica_groups=mesh['gossip'=16,'mp'=2] {'gossip'}, dimensions={0}, use_global_device_ids=true | all-gather | bytes 136 | tf_op jit(solution)/shard_map/all_gather | solution.py:33
  89.4 7.5 %all-reduce.5.cloned.1.call-done = f32[1024,64]{0,1:T(8,128)} async-done(((f32[1024,64]{0,1:T(8,128)}), f32[1024,64]{0,1:T(8,128)}) %all-reduce.5.cloned.1.call-update) | async-done | bytes 262160 | tf_op jit(solution)/shard_map/psum | solution.py:45
  96.9 1.0 fusion.18
  97.9 0.2 copy.25
  98.0 0.2 all_to_all.38
  98.2 0.5 broadcast.54
  98.7 1.4 reduce.6
  100.1 0.7 reshape.71
  100.8 6.1 %all-to-all-start = ((bf16[16,2,2048]{2,1,0:T(2,128)(2,1)}), bf16[16,2,2048]{2,1,0:T(2,128)(2,1)S(1)}, u32[]{:S(2)}, u32[]{:S(2)}) async-start(bf16[16,2,2048]{2,1,0:T(2,128)(2,1)} %reshape.71), calls=%async_computation | async-start | bytes 262144 | tf_op jit(solution)/shard_map/all_to_all | solution.py:18
  106.9 4.8 %all-to-all-done = bf16[16,2,2048]{2,1,0:T(2,128)(2,1)S(1)} async-done(((bf16[16,2,2048]{2,1,0:T(2,128)(2,1)}), bf16[16,2,2048]{2,1,0:T(2,128)(2,1)S(1)}, u32[]{:S(2)}, u32[]{:S(2)}) %all-to-all-start) | async-done | bytes 131104 | tf_op jit(solution)/shard_map/all_to_all | solution.py:18
  111.7 0.1 reshape.72
  111.8 0.2 copy.38
  112.0 0.6 gather_fusion
  112.7 0.7 reduce.7
  113.4 0.7 reshape.73
  114.1 6.5 %all-to-all-start.1 = ((bf16[16,2,2048]{2,1,0:T(2,128)(2,1)}), bf16[16,2,2048]{2,1,0:T(2,128)(2,1)S(1)}, u32[]{:S(2)}, u32[]{:S(2)}) async-start(bf16[16,2,2048]{2,1,0:T(2,128)(2,1)} %reshape.73), calls=%async_computation.1 | async-start | bytes 262144 | tf_op jit(solution)/shard_map/all_to_all | solution.py:20
  120.7 5.7 %fusion.20 = f32[1024,2048]{1,0:T(8,128)} fusion(bf16[1024,64]{0,1:T(8,128)(2,1)S(1)} %fusion.18, f32[2048,64]{0,1:T(8,128)S(1)} %copy-done), kind=kOutput, calls=%fused_computation.46 | convolution fusion | flops 1610612736 | bytes 9043968 | tf_op jit(solution)/shard_map/dot_general | solution.py:44
  126.5 0.7 convert_reduce_fusion.1
  127.2 0.2 reshape.41
  127.4 0.2 copy.28
  127.6 14.2 %multiply_reduce_fusion.1 = (f32[]{:T(128)}, f32[1024,2048]{1,0:T(8,128)S(1)}) fusion(bf16[2,1,1024,2048]{3,2,1,0:T(8,128)(2,1)} %param.9, f32[]{:T(128)S(6)} %min.7, f32[]{:T(128)S(6)} %min.6, f32[1,1024,2048]{2,1,0:T(8,128)} %param.7, f32[2048,64]{0,1:T(8,128)S(1)} %copy-done, f32[1024,64]{0,1:T(8,128)S(1)} %copy.28, bf16[1024,64]{0,1:T(8,128)(2,1)S(1)} %fusion.18), kind=kOutput, calls=%fused_computation.13 | convolution fusion | flops 1631715328 | bytes 26083340 | tf_op jit(solution)/shard_map/dot_general | solution.py:49
  141.9 3.4 %copy-done.1 = f32[1024,2048]{1,0:T(8,128)} copy-done((f32[1024,2048]{1,0:T(8,128)}, f32[1024,2048]{1,0:T(8,128)S(1)}, u32[]{:S(2)}) %copy-start.1) | copy-done | bytes 8388632
  145.2 11.4 %fusion.6 = f32[1024,64]{0,1:T(8,128)} fusion(f32[2048,64]{0,1:T(8,128)S(1)} %copy-done, f32[1024,2048]{1,0:T(8,128)S(1)} %get-tuple-element.18, f32[1024,2048]{1,0:T(8,128)} %fusion.20), kind=kOutput, calls=%fused_computation.15 | convolution fusion | flops 1612709888 | bytes 17563648 | tf_op jit(solution)/shard_map/dot_general | solution.py:45
  156.7 23.5 %all-reduce.7.cloned.1.call-done = f32[1024,64]{0,1:T(8,128)} async-done(((f32[1024,64]{0,1:T(8,128)}), f32[1024,64]{0,1:T(8,128)}) %all-reduce.7.cloned.1.call-update) | async-done | bytes 262160 | tf_op jit(solution)/shard_map/psum | solution.py:45
  180.2 1.7 convert_bitcast_fusion
  181.8 0.2 copy.29
  182.0 0.2 all_to_all.39
  182.2 1.4 reduce.8
  183.6 0.7 reshape.75
  184.3 6.1 %all-to-all-start.2 = ((bf16[16,2,2048]{2,1,0:T(2,128)(2,1)}), bf16[16,2,2048]{2,1,0:T(2,128)(2,1)S(1)}, u32[]{:S(2)}, u32[]{:S(2)}) async-start(bf16[16,2,2048]{2,1,0:T(2,128)(2,1)} %reshape.75), calls=%async_computation.2 | async-start | bytes 262144 | tf_op jit(solution)/shard_map/all_to_all | solution.py:18
  190.3 4.8 %all-to-all-done.2 = bf16[16,2,2048]{2,1,0:T(2,128)(2,1)S(1)} async-done(((bf16[16,2,2048]{2,1,0:T(2,128)(2,1)}), bf16[16,2,2048]{2,1,0:T(2,128)(2,1)S(1)}, u32[]{:S(2)}, u32[]{:S(2)}) %all-to-all-start.2) | async-done | bytes 131104 | tf_op jit(solution)/shard_map/all_to_all | solution.py:18
  195.3 0.2 copy.37
  195.4 0.6 gather_fusion.1
  196.1 0.7 reduce.9
  196.8 0.7 reshape.77
  197.5 6.5 %all-to-all-start.3 = ((bf16[16,2,2048]{2,1,0:T(2,128)(2,1)}), bf16[16,2,2048]{2,1,0:T(2,128)(2,1)S(1)}, u32[]{:S(2)}, u32[]{:S(2)}) async-start(bf16[16,2,2048]{2,1,0:T(2,128)(2,1)} %reshape.77), calls=%async_computation.3 | async-start | bytes 262144 | tf_op jit(solution)/shard_map/all_to_all | solution.py:20
  204.1 0.6 pad_maximum_fusion.1
  204.6 4.3 %all-to-all-done.3 = bf16[16,2,2048]{2,1,0:T(2,128)(2,1)S(1)} async-done(((bf16[16,2,2048]{2,1,0:T(2,128)(2,1)}), bf16[16,2,2048]{2,1,0:T(2,128)(2,1)S(1)}, u32[]{:S(2)}, u32[]{:S(2)}) %all-to-all-start.3) | async-done | bytes 131104 | tf_op jit(solution)/shard_map/all_to_all | solution.py:20
  209.0 0.7 convert_reduce_fusion
  209.8 0.2 reshape.42
  210.0 0.2 copy.32
  210.2 13.3 %multiply_reduce_fusion = (f32[]{:T(128)}, f32[1,1024,2048]{2,1,0:T(8,128)}) fusion(f32[1024,2048]{1,0:T(8,128)} %copy-done.1, f32[2048,64]{0,1:T(8,128)S(1)} %copy-done, f32[1024,64]{0,1:T(8,128)S(1)} %copy.32, bf16[1024,64]{0,1:T(8,128)(2,1)S(1)} %get-tuple-element.12), kind=kOutput, calls=%fused_computation.12 | convolution fusion | flops 1619132416 | bytes 17694724 | tf_op jit(solution)/shard_map/dot_general | solution.py:49
  223.5 42.2 %all-reduce = (f32[]{:T(128)}, f32[]{:T(128)}) all-reduce(f32[]{:T(128)} %get-tuple-element.19, f32[]{:T(128)} %get-tuple-element.17), channel_id=1, replica_groups=mesh['gossip'=16,'mp'=2] {'gossip','mp'}, use_global_device_ids=true, to_apply=%region_9.11 | all-reduce | flops 2 | bytes 16 | tf_op jit(solution)/shard_map/psum | solution.py:52
  267.0 0.6 pad_maximum_fusion
  (21 shorter events, 0.8 us)
Async XLA Ops:
  7.2 47.6 %copy-start = (f32[2048,64]{0,1:T(8,128)S(1)}, f32[2048,64]{0,1:T(8,128)}, u32[]{:S(2)}) copy-start(f32[2048,64]{0,1:T(8,128)} %param.10) | copy-start | bytes 1572868
  7.2 47.6 %copy-start.2 = (f32[1,1024,64]{1,2,0:T(8,128)S(1)}, f32[1,1024,64]{1,2,0:T(8,128)}, u32[]{:S(2)}) copy-start(f32[1,1024,64]{1,2,0:T(8,128)} %param.8) | copy-start | bytes 786436
  7.2 89.7 %all-reduce.5.cloned.1.call-start = ((), (), s32[]{:S(2)}) async-start(), calls=%async_computation.4 | async-start | bytes 524288 | tf_op jit(solution)/shard_map/psum | solution.py:45
  61.5 13.6 %copy-start.3 = (s32[2,1]{0,1:T(1,128)S(1)}, s32[2,1]{0,1:T(1,128)}, u32[]{:S(2)}) copy-start(s32[2,1]{0,1:T(1,128)} %param.11) | copy-start | bytes 28
  100.8 10.9 %all-to-all-start = ((bf16[16,2,2048]{2,1,0:T(2,128)(2,1)}), bf16[16,2,2048]{2,1,0:T(2,128)(2,1)S(1)}, u32[]{:S(2)}, u32[]{:S(2)}) async-start(bf16[16,2,2048]{2,1,0:T(2,128)(2,1)} %reshape.71), calls=%async_computation | async-start | bytes 262144 | tf_op jit(solution)/shard_map/all_to_all | solution.py:18
  114.1 12.2 %all-to-all-start.1 = ((bf16[16,2,2048]{2,1,0:T(2,128)(2,1)}), bf16[16,2,2048]{2,1,0:T(2,128)(2,1)S(1)}, u32[]{:S(2)}, u32[]{:S(2)}) async-start(bf16[16,2,2048]{2,1,0:T(2,128)(2,1)} %reshape.73), calls=%async_computation.1 | async-start | bytes 262144 | tf_op jit(solution)/shard_map/all_to_all | solution.py:20
  120.6 59.5 %all-reduce.7.cloned.1.call-start = ((), (), s32[]{:S(2)}) async-start(), calls=%async_computation.5 | async-start | bytes 524288 | tf_op jit(solution)/shard_map/psum | solution.py:45
  141.9 3.4 %copy-start.1 = (f32[1024,2048]{1,0:T(8,128)}, f32[1024,2048]{1,0:T(8,128)S(1)}, u32[]{:S(2)}) copy-start(f32[1024,2048]{1,0:T(8,128)S(1)} %get-tuple-element.18) | copy-start | bytes 25165828
  184.3 10.9 %all-to-all-start.2 = ((bf16[16,2,2048]{2,1,0:T(2,128)(2,1)}), bf16[16,2,2048]{2,1,0:T(2,128)(2,1)S(1)}, u32[]{:S(2)}, u32[]{:S(2)}) async-start(bf16[16,2,2048]{2,1,0:T(2,128)(2,1)} %reshape.75), calls=%async_computation.2 | async-start | bytes 262144 | tf_op jit(solution)/shard_map/all_to_all | solution.py:18
  197.5 11.4 %all-to-all-start.3 = ((bf16[16,2,2048]{2,1,0:T(2,128)(2,1)}), bf16[16,2,2048]{2,1,0:T(2,128)(2,1)S(1)}, u32[]{:S(2)}, u32[]{:S(2)}) async-start(bf16[16,2,2048]{2,1,0:T(2,128)(2,1)} %reshape.77), calls=%async_computation.3 | async-start | bytes 262144 | tf_op jit(solution)/shard_map/all_to_all | solution.py:20
Sparse Core Ops, SparseCore 0:
  74.6 22.2 all-reduce.4
  156.8 23.2 all-reduce.6
where the time goes:
time: 275 us; the launch traced here: 274 us
  blocking collectives  97.9 us (36%)
  matrix products  64.2 us (23%)
  waiting for transfers between devices  44.8 us (16%)
  starting transfers between devices  25.2 us (9%)
  between operations  17.1 us (6%)
  other arithmetic  14.8 us (5%)
  local copies, waits for them, and re-layouts  10.4 us (4%)
    psum x1, blocking collectives, body(): drift_list.append(lax.psum(local_drift, ('gossip', 'mp')) / total)  42.2 us
    psum x1, blocking collectives, body(): squares = lax.psum(local_squares, ('gossip', 'mp'))  41.6 us
    psum x2, waiting for transfers between devices, body(): lax.psum(jnp.dot(half - rebuilt, projection, precision=highest), 'mp')  31 us
    dot_general x2, matrix products, body(): jnp.dot(mate.astype(jnp.float32) - public_state, projection.T, precision=...  27.6 us
    dot_general x2, matrix products, body(): jnp.dot(half - rebuilt, projection, precision=highest)  24.3 us
    all_gather x1, blocking collectives, body(): whole_table = lax.all_gather(partners, 'gossip', axis=1, tiled=True)  14.1 us
    all_to_all x2, starting transfers between devices, partner_rows(): lax.all_to_all(reordered, 'gossip', split_axis=0, concat_axis=0, tiled=True)  13 us
    dot_general x2, matrix products, body(): rebuilt = jnp.dot(coef_rows, projection.T, precision=highest)  12.4 us
  transfers between devices with their start and end apart: 6, of which 5 were waited for; matrix products, arithmetic and copies ran while one was open for 2% of the time, Pallas kernels for 0%

commit v1 on v0

--- a/solution.py
+++ b/solution.py
@@ -42,7 +42,9 @@
         table_row = whole_table[round_index]
         coef_rows = public_state
         rebuilt = jnp.dot(coef_rows, projection.T, precision=highest)
-        summed = lax.psum(jnp.dot(half - rebuilt, projection, precision=highest), "mp")
+        part = jnp.dot(half - rebuilt, projection, precision=highest)
+        parts = lax.all_gather(part, "mp")
+        summed = jnp.sum(parts, axis=0)
         sent = (public_state + summed).astype(jnp.bfloat16)
         mate = partner_rows(sent, table_row)
         public_state = sent.astype(jnp.float32)

time: 275 us -> 246 us (0.89)
  waiting for transfers between devices: 44.8 us -> 8.32 us
  blocking collectives: 97.9 us -> 116 us
  between operations: 17.1 us -> 3.74 us
  matrix products: 64.2 us -> 69.2 us
    psum x2 -> x0, waiting for transfers between devices: 31 us -> none  [body(): lax.psum(jnp.dot(half - rebuilt, projection, precision=highest), 'mp')]
    all_gather x0 -> x2, blocking collectives: none -> 16.3 us  [body(): parts = lax.all_gather(part, 'mp')]
    all_to_all x2, waiting for transfers between devices: 9.58 us -> 4.22 us  [partner_rows(): lax.all_to_all(pieces, 'gossip', split_axis=0, concat_axis=0, tiled=True)]
    all_to_all x2, starting transfers between devices: 13 us -> 16.3 us  [partner_rows(): lax.all_to_all(reordered, 'gossip', split_axis=0, concat_axis=0, tiled=True)]
    unnamed x18 -> x19, local copies, waits for them, and re-layouts: 7.09 us -> 3.92 us
    dot_general x2, matrix products: 24.3 us -> 27.1 us  [body(): part = jnp.dot(half - rebuilt, projection, precision=highest)]
    all_to_all x2 -> x0, other arithmetic: 2.75 us -> none  [partner_rows(): lax.all_to_all(pieces, 'gossip', split_axis=0, concat_axis=0, tiled=True)]
  transfers between devices with their start and end apart: 6 -> 4, of which waited for: 5 -> 2; matrix products, arithmetic and copies ran while one was open for 2% -> 3% of each run, Pallas kernels for 0% -> 0%
where the time goes in v1:
time: 246 us; the launch traced here: 245 us
  blocking collectives  116 us (47%)
  matrix products  69.2 us (28%)
  starting transfers between devices  27.4 us (11%)
  other arithmetic  12.5 us (5%)
  local copies, waits for them, and re-layouts  8.39 us (3%)
  waiting for transfers between devices  8.32 us (3%)
  between operations  3.74 us (2%)
    psum x1, blocking collectives, body(): drift_list.append(lax.psum(local_drift, ('gossip', 'mp')) / total)  42.2 us
    psum x1, blocking collectives, body(): squares = lax.psum(local_squares, ('gossip', 'mp'))  41.6 us
    dot_general x2, matrix products, body(): jnp.dot(mate.astype(jnp.float32) - public_state, projection.T, precision=...  27.5 us
    dot_general x2, matrix products, body(): part = jnp.dot(half - rebuilt, projection, precision=highest)  27.1 us
    all_to_all x2, starting transfers between devices, partner_rows(): lax.all_to_all(reordered, 'gossip', split_axis=0, concat_axis=0, tiled=True)  16.3 us
    all_gather x2, blocking collectives, body(): parts = lax.all_gather(part, 'mp')  16.3 us
    all_gather x1, blocking collectives, body(): whole_table = lax.all_gather(partners, 'gossip', axis=1, tiled=True)  15.6 us
    dot_general x2, matrix products, body(): rebuilt = jnp.dot(coef_rows, projection.T, precision=highest)  14.6 us
  transfers between devices with their start and end apart: 4, of which 2 were waited for; matrix products, arithmetic and copies ran while one was open for 3% of the time, Pallas kernels for 0%

profile of v1, /device:TPU:12, one launch (start us, length us, event | category | flops | bytes accessed | tf_op | source)
XLA Modules:
  0.0 245.2 jit_solution(8556378105193198797)
XLA Ops:
  0.7 5.2 %fusion.3 = (f32[]{:T(128)}, f32[]{:T(128)}) fusion(bf16[2,1,1024,2048]{3,2,1,0:T(8,128)(2,1)} %param.9), kind=kLoop, calls=%fused_computation.9 | loop fusion | flops 12582910 | bytes 8388616 | tf_op jit(solution)/shard_map/reduce_sum | solution.py:36
  5.9 41.6 %all-reduce.1 = (f32[]{:T(128)}, f32[]{:T(128)}) all-reduce(f32[]{:T(128)} %get-tuple-element.10, f32[]{:T(128)} %get-tuple-element.9), channel_id=1, replica_groups=mesh['gossip'=16,'mp'=2] {'gossip','mp'}, use_global_device_ids=true, to_apply=%region_1.0 | all-reduce | flops 2 | bytes 16 | tf_op jit(solution)/shard_map/psum | solution.py:37
  48.2 0.2 copy.31
  48.4 0.2 squeeze.17
  48.6 9.0 %fusion.17 = f32[1024,2048]{1,0:T(8,128)} fusion(f32[2048,64]{0,1:T(8,128)S(1)} %copy-done, f32[1,1024,64]{1,2,0:T(8,128)S(1)} %copy-done.2), kind=kOutput, calls=%fused_computation.30 | convolution fusion | flops 1610612736 | bytes 9175040 | tf_op jit(solution)/shard_map/dot_general | solution.py:44
  57.6 13.3 %fusion.8 = f32[1024,64]{0,1:T(8,128)S(1)} fusion(f32[2048,64]{0,1:T(8,128)S(1)} %copy-done, f32[1024,2048]{1,0:T(8,128)} %fusion.17, f32[1,1024,2048]{2,1,0:T(8,128)} %param.7, f32[]{:T(128)S(6)} %min.6, bf16[2,1,1024,2048]{3,2,1,0:T(8,128)(2,1)} %param.9), kind=kOutput, calls=%fused_computation.17 | convolution fusion | flops 1619001344 | bytes 21757956 | tf_op jit(solution)/shard_map/dot_general | solution.py:45
  71.0 7.0 %all-gather = f32[2048,64]{0,1:T(8,128)S(1)} all-gather(f32[1024,64]{0,1:T(8,128)S(1)} %fusion.8), channel_id=2, replica_groups=mesh['gossip'=16,'mp'=2] {'mp'}, dimensions={0}, use_global_device_ids=true | all-gather | bytes 786432 | tf_op jit(solution)/shard_map/all_gather | solution.py:46
  78.0 0.4 reshape.108
  78.5 0.6 reduce_sum.63
  79.1 0.2 copy.32
  79.3 0.2 reduce_sum.64
  79.5 0.5 broadcast.54
  80.0 0.6 reduce.6
  80.6 0.7 reshape.122
  81.4 5.0 %all-to-all-start = ((bf16[16,2,2048]{2,1,0:T(2,128)(2,1)}), bf16[16,2,2048]{2,1,0:T(2,128)(2,1)S(1)}, u32[]{:S(2)}, u32[]{:S(2)}) async-start(bf16[16,2,2048]{2,1,0:T(2,128)(2,1)} %reshape.122), calls=%async_computation | async-start | bytes 262144 | tf_op jit(solution)/shard_map/all_to_all | solution.py:18
  86.4 15.6 %all-gather.2 = s32[16,1,2]{2,1,0:T(1,128)S(1)} all-gather(s32[1,1,2]{2,1,0:T(1,128)S(1)} %bitcast.80), channel_id=1, replica_groups=mesh['gossip'=16,'mp'=2] {'gossip'}, dimensions={0}, use_global_device_ids=true | all-gather | bytes 136 | tf_op jit(solution)/shard_map/all_gather | solution.py:33
  103.2 0.6 gather_fusion
  103.9 0.6 reduce.7
  104.5 0.7 reshape.124
  105.2 9.8 %all-to-all-start.1 = ((bf16[16,2,2048]{2,1,0:T(2,128)(2,1)}), bf16[16,2,2048]{2,1,0:T(2,128)(2,1)S(1)}, u32[]{:S(2)}, u32[]{:S(2)}) async-start(bf16[16,2,2048]{2,1,0:T(2,128)(2,1)} %reshape.124), calls=%async_computation.1 | async-start | bytes 262144 | tf_op jit(solution)/shard_map/all_to_all | solution.py:20
  115.0 5.7 %fusion.27 = f32[1024,2048]{1,0:T(8,128)} fusion(bf16[1024,64]{0,1:T(8,128)(2,1)S(1)} %fusion.19, f32[2048,64]{0,1:T(8,128)S(1)} %copy-done), kind=kOutput, calls=%fused_computation.53 | convolution fusion | flops 1610612736 | bytes 9043968 | tf_op jit(solution)/shard_map/dot_general | solution.py:44
  120.8 0.7 convert_reduce_fusion.1
  121.5 0.2 reshape.90
  121.7 0.2 copy.35
  121.9 14.2 %multiply_reduce_fusion.1 = (f32[]{:T(128)}, f32[1024,2048]{1,0:T(8,128)S(1)}) fusion(bf16[2,1,1024,2048]{3,2,1,0:T(8,128)(2,1)} %param.9, f32[]{:T(128)S(6)} %min.7, f32[]{:T(128)S(6)} %min.6, f32[1,1024,2048]{2,1,0:T(8,128)} %param.7, f32[2048,64]{0,1:T(8,128)S(1)} %copy-done, f32[1024,64]{0,1:T(8,128)S(1)} %copy.35, bf16[1024,64]{0,1:T(8,128)(2,1)S(1)} %fusion.19), kind=kOutput, calls=%fused_computation.13 | convolution fusion | flops 1631715328 | bytes 26083340 | tf_op jit(solution)/shard_map/dot_general | solution.py:51
  136.1 13.7 %fusion.6 = f32[1024,64]{0,1:T(8,128)S(1)} fusion(f32[2048,64]{0,1:T(8,128)S(1)} %copy-done, f32[1024,2048]{1,0:T(8,128)S(1)} %get-tuple-element.20, f32[1024,2048]{1,0:T(8,128)} %fusion.27), kind=kOutput, calls=%fused_computation.15 | convolution fusion | flops 1612709888 | bytes 17563648 | tf_op jit(solution)/shard_map/dot_general | solution.py:45
  149.9 9.2 %all-gather.1 = f32[2048,64]{0,1:T(8,128)S(1)} all-gather(f32[1024,64]{0,1:T(8,128)S(1)} %fusion.6), channel_id=3, replica_groups=mesh['gossip'=16,'mp'=2] {'mp'}, dimensions={0}, use_global_device_ids=true | all-gather | bytes 786432 | tf_op jit(solution)/shard_map/all_gather | solution.py:46
  159.1 0.4 reshape.109
  159.5 0.6 reduce_sum.66
  160.2 0.2 copy.36
  160.4 0.2 reduce_sum.67
  160.6 0.6 reduce.8
  161.2 0.7 reshape.126
  161.9 6.1 %all-to-all-start.2 = ((bf16[16,2,2048]{2,1,0:T(2,128)(2,1)}), bf16[16,2,2048]{2,1,0:T(2,128)(2,1)S(1)}, u32[]{:S(2)}, u32[]{:S(2)}) async-start(bf16[16,2,2048]{2,1,0:T(2,128)(2,1)} %reshape.126), calls=%async_computation.2 | async-start | bytes 262144 | tf_op jit(solution)/shard_map/all_to_all | solution.py:18
  168.0 0.6 pad_maximum_fusion.1
  168.6 4.2 %all-to-all-done.2 = bf16[16,2,2048]{2,1,0:T(2,128)(2,1)S(1)} async-done(((bf16[16,2,2048]{2,1,0:T(2,128)(2,1)}), bf16[16,2,2048]{2,1,0:T(2,128)(2,1)S(1)}, u32[]{:S(2)}, u32[]{:S(2)}) %all-to-all-start.2) | async-done | bytes 131104 | tf_op jit(solution)/shard_map/all_to_all | solution.py:18
  173.1 0.6 gather_fusion.1
  173.8 0.6 reduce.9
  174.4 0.7 reshape.128
  175.1 6.5 %all-to-all-start.3 = ((bf16[16,2,2048]{2,1,0:T(2,128)(2,1)}), bf16[16,2,2048]{2,1,0:T(2,128)(2,1)S(1)}, u32[]{:S(2)}, u32[]{:S(2)}) async-start(bf16[16,2,2048]{2,1,0:T(2,128)(2,1)} %reshape.128), calls=%async_computation.3 | async-start | bytes 262144 | tf_op jit(solution)/shard_map/all_to_all | solution.py:20
  181.6 0.7 fusion.23
  182.4 4.1 %all-to-all-done.3 = bf16[16,2,2048]{2,1,0:T(2,128)(2,1)S(1)} async-done(((bf16[16,2,2048]{2,1,0:T(2,128)(2,1)}), bf16[16,2,2048]{2,1,0:T(2,128)(2,1)S(1)}, u32[]{:S(2)}, u32[]{:S(2)}) %all-to-all-start.3) | async-done | bytes 131104 | tf_op jit(solution)/shard_map/all_to_all | solution.py:20
  186.6 0.7 convert_reduce_fusion
  187.3 0.2 reshape.91
  187.6 0.2 copy.39
  187.7 13.3 %multiply_reduce_fusion = (f32[]{:T(128)}, f32[1,1024,2048]{2,1,0:T(8,128)}) fusion(f32[1024,2048]{1,0:T(8,128)} %copy-done.1, f32[2048,64]{0,1:T(8,128)S(1)} %copy-done, f32[1024,64]{0,1:T(8,128)S(1)} %copy.39, f32[1024,64]{0,1:T(8,128)S(1)} %reduce_sum.66, bf16[1024,64]{0,1:T(8,128)(2,1)S(1)} %fusion.19), kind=kOutput, calls=%fused_computation.12 | convolution fusion | flops 1619329024 | bytes 17956868 | tf_op jit(solution)/shard_map/dot_general | solution.py:51
  201.1 42.2 %all-reduce = (f32[]{:T(128)}, f32[]{:T(128)}) all-reduce(f32[]{:T(128)} %get-tuple-element.21, f32[]{:T(128)} %get-tuple-element.19), channel_id=1, replica_groups=mesh['gossip'=16,'mp'=2] {'gossip','mp'}, use_global_device_ids=true, to_apply=%region_9.11 | all-reduce | flops 2 | bytes 16 | tf_op jit(solution)/shard_map/psum | solution.py:54
  244.6 0.6 pad_maximum_fusion
  (25 shorter events, 1.2 us)
Async XLA Ops:
  0.6 48.0 %copy-start = (f32[2048,64]{0,1:T(8,128)S(1)}, f32[2048,64]{0,1:T(8,128)}, u32[]{:S(2)}) copy-start(f32[2048,64]{0,1:T(8,128)} %param.10) | copy-start | bytes 1572868
  0.6 47.5 %copy-start.2 = (f32[1,1024,64]{1,2,0:T(8,128)S(1)}, f32[1,1024,64]{1,2,0:T(8,128)}, u32[]{:S(2)}) copy-start(f32[1,1024,64]{1,2,0:T(8,128)} %param.8) | copy-start | bytes 786436
  57.6 28.8 %copy-start.3 = (s32[2,1]{0,1:T(1,128)S(1)}, s32[2,1]{0,1:T(1,128)}, u32[]{:S(2)}) copy-start(s32[2,1]{0,1:T(1,128)} %param.11) | copy-start | bytes 28
  81.4 21.5 %all-to-all-start = ((bf16[16,2,2048]{2,1,0:T(2,128)(2,1)}), bf16[16,2,2048]{2,1,0:T(2,128)(2,1)S(1)}, u32[]{:S(2)}, u32[]{:S(2)}) async-start(bf16[16,2,2048]{2,1,0:T(2,128)(2,1)} %reshape.122), calls=%async_computation | async-start | bytes 262144 | tf_op jit(solution)/shard_map/all_to_all | solution.py:18
  105.2 15.4 %all-to-all-start.1 = ((bf16[16,2,2048]{2,1,0:T(2,128)(2,1)}), bf16[16,2,2048]{2,1,0:T(2,128)(2,1)S(1)}, u32[]{:S(2)}, u32[]{:S(2)}) async-start(bf16[16,2,2048]{2,1,0:T(2,128)(2,1)} %reshape.124), calls=%async_computation.1 | async-start | bytes 262144 | tf_op jit(solution)/shard_map/all_to_all | solution.py:20
  136.1 13.8 %copy-start.1 = (f32[1024,2048]{1,0:T(8,128)}, f32[1024,2048]{1,0:T(8,128)S(1)}, u32[]{:S(2)}) copy-start(f32[1024,2048]{1,0:T(8,128)S(1)} %get-tuple-element.20) | copy-start | bytes 25165828
  161.9 10.9 %all-to-all-start.2 = ((bf16[16,2,2048]{2,1,0:T(2,128)(2,1)}), bf16[16,2,2048]{2,1,0:T(2,128)(2,1)S(1)}, u32[]{:S(2)}, u32[]{:S(2)}) async-start(bf16[16,2,2048]{2,1,0:T(2,128)(2,1)} %reshape.126), calls=%async_computation.2 | async-start | bytes 262144 | tf_op jit(solution)/shard_map/all_to_all | solution.py:18
  175.1 11.4 %all-to-all-start.3 = ((bf16[16,2,2048]{2,1,0:T(2,128)(2,1)}), bf16[16,2,2048]{2,1,0:T(2,128)(2,1)S(1)}, u32[]{:S(2)}, u32[]{:S(2)}) async-start(bf16[16,2,2048]{2,1,0:T(2,128)(2,1)} %reshape.128), calls=%async_computation.3 | async-start | bytes 262144 | tf_op jit(solution)/shard_map/all_to_all | solution.py:20
